TPU v7x, 32 devices: a whole 2x2x4 slice. The times are simulated.
32 devices in a mesh: groups: 2 (over x), cells: 16 (over z, y, core).
Axes of the slice: x: 2, y: 2, z: 4, core: 2. Of those that a mesh axis runs over, the one named last changes fastest.
Arguments:
- pair_act: bfloat16 [768, 384, 128], P(('groups', 'cells')), parts along dimension 0, may hold values from -6 to 6
- pair_mask: int32 [768, 384], P(('groups', 'cells')), parts along dimension 0, may hold values from 0 to 1, as said below
- chain_ids: int32 [768], P('groups'), parts along dimension 0, may hold values from 0 to 3, never falling along the last dimension, each value on 1 to 192 neighbouring positions
- proj_weight: bfloat16 [128, 256], replicated, may hold values from -0.5 to 0.5
- gate_weight: bfloat16 [128, 128], replicated, may hold values from -0.5 to 0.5
- chain_bias: float32 [2, 128], replicated, may hold values from -4 to 4
- out_weight: bfloat16 [64, 128], replicated, may hold values from -0.75 to 0.75
- out_grad: bfloat16 [768, 384, 128], P(('groups', 'cells')), parts along dimension 0, may hold values from -6 to 6
Outputs:
- pair_grad: bfloat16 [768, 384, 128], P(('groups', 'cells')), parts along dimension 0
- proj_weight_grad: float32 [256, 256], P('groups'), parts along dimension 0
- gate_weight_grad: float32 [256, 128], P('groups'), parts along dimension 0
- out_weight_grad: float32 [128, 128], P('groups'), parts along dimension 0
There are 2 independent parts, one for each index of `groups`. A program takes and returns all parts, laid end to end along the dimension named above; an argument that names none is the same for every part. Nothing has to cross between parts.
Inputs may be any that keep to these rules, and one draw needn't show every extreme that they name: pair_mask[i, j] = valid[i] * valid[j] for a 0 or 1 validity of each residue.
All inputs are finite; a program needn't handle non-finite values.
Results may differ from a plain program's by a relative error of at most 0.012.
Values may be sent and summed in bfloat16 or wider, within the bound.
No kernel may reach another device: no remote copies, remote signals or barrier semaphores. Data moves between devices by JAX's collectives and lax.ppermute only.
A program may use at most 64 MiB of HBM per device.

v0:
```python
import jax
import jax.numpy as jnp
from jax import lax
from jax.sharding import PartitionSpec as P

EPS = 1e-05


def normalize_axis(values, axis):
    center = values - jnp.mean(values, axis=axis, keepdims=True)
    scale = lax.rsqrt(jnp.mean(center * center, axis=axis, keepdims=True) + EPS)
    return (center * scale, scale)


def norm_backward(grad, normed, scale, axis):
    first = jnp.mean(grad, axis=axis, keepdims=True)
    second = jnp.mean(grad * normed, axis=axis, keepdims=True)
    return scale * (grad - first - normed * second)


def local(
    pair_act, pair_mask, chain_ids, proj_weight, gate_weight, chain_bias, out_weight, out_grad
):
    devices = lax.axis_size("cells")
    rows_here = pair_act.shape[0]
    length = pair_act.shape[1]
    width = pair_act.shape[2]
    hidden = out_weight.shape[0]
    halfway = length // 2
    channel_pairs = devices // 2
    per_device = 2 * hidden // devices
    count = rows_here * length
    zfull = pair_act.astype(jnp.float32).reshape(count, width)
    zhat, zscale = normalize_axis(zfull, 1)
    normed = zhat.astype(jnp.bfloat16)
    projected = jnp.einsum("xc,cf->fx", normed, proj_weight, preferred_element_type=jnp.float32)
    keeper = pair_mask.astype(jnp.float32).reshape(1, count)
    values = projected[: 2 * hidden]
    sigma = jax.nn.sigmoid(projected[2 * hidden :])
    factors = (keeper * sigma * values).astype(jnp.bfloat16)
    outgoing = factors.reshape(2, channel_pairs, per_device, rows_here, 2, halfway)
    outgoing = jnp.transpose(outgoing, (1, 4, 0, 2, 3, 5)).reshape(
        devices, 2, per_device, rows_here, halfway
    )
    arrived = lax.all_to_all(outgoing, "cells", split_axis=0, concat_axis=3, tiled=True)
    left_half = arrived[0, 0]
    right_half = arrived[0, 1]
    partial_value = jnp.einsum(
        "cik,cjk->cij", left_half, right_half, preferred_element_type=jnp.float32
    )
    landed = lax.all_to_all(
        partial_value.reshape(per_device, devices, rows_here, length).astype(jnp.bfloat16),
        "cells",
        split_axis=1,
        concat_axis=0,
        tiled=True,
    ).astype(jnp.float32)
    landed = landed.reshape(channel_pairs, 2, per_device, rows_here, length)
    triangle = jnp.sum(landed, axis=1).reshape(hidden, count)
    tri_hat, tri_scale = normalize_axis(triangle, 0)
    tri_low = tri_hat.astype(jnp.bfloat16)
    outputs = jnp.einsum("hx,hc->xc", tri_low, out_weight, preferred_element_type=jnp.float32)
    start = lax.axis_index("cells") * rows_here
    own_chain = lax.dynamic_slice_in_dim(chain_ids, start, rows_here, 0)
    same_chain = (own_chain[:, None] == chain_ids[None, :]).reshape(count, 1)
    logits = jnp.dot(normed, gate_weight, preferred_element_type=jnp.float32)
    logits = logits + jnp.where(same_chain, chain_bias[0][None, :], chain_bias[1][None, :])
    gating = jax.nn.sigmoid(logits)
    upstream = out_grad.reshape(count, width).astype(jnp.float32)
    d_outputs = (upstream * gating).astype(jnp.bfloat16)
    d_logits = (upstream * outputs * gating * (1.0 - gating)).astype(jnp.bfloat16)
    out_term = jnp.einsum("hx,xc->hc", tri_low, d_outputs, preferred_element_type=jnp.float32)
    gate_term = jnp.einsum("xc,xd->cd", normed, d_logits, preferred_element_type=jnp.float32)
    d_hat = jnp.einsum("xc,hc->hx", d_outputs, out_weight, preferred_element_type=jnp.float32)
    d_tri = norm_backward(d_hat, tri_hat, tri_scale, 0).astype(jnp.bfloat16)
    doubled = jnp.broadcast_to(
        d_tri.reshape(channel_pairs, 1, per_device, rows_here, length),
        (channel_pairs, 2, per_device, rows_here, length),
    )
    whole = lax.all_to_all(
        doubled.reshape(devices, per_device, rows_here, length),
        "cells",
        split_axis=0,
        concat_axis=2,
        tiled=True,
    )[0]
    d_left = jnp.einsum("cij,cjk->cik", whole, right_half, preferred_element_type=jnp.float32)
    d_right = jnp.einsum("cij,cik->cjk", whole, left_half, preferred_element_type=jnp.float32)
    d_pair = jnp.stack([d_left, d_right]).astype(jnp.bfloat16)
    returned = lax.all_to_all(
        d_pair.reshape(2, per_device, devices, rows_here, halfway),
        "cells",
        split_axis=2,
        concat_axis=2,
        tiled=True,
    )
    returned = returned.reshape(2, per_device, channel_pairs, 2, rows_here, halfway)
    d_factors = (
        jnp.transpose(returned, (0, 2, 1, 4, 3, 5)).reshape(2 * hidden, count).astype(jnp.float32)
    )
    d_values = d_factors * keeper * sigma
    d_gates = d_factors * keeper * values * sigma * (1.0 - sigma)
    d_proj = jnp.concatenate([d_values, d_gates], axis=0).astype(jnp.bfloat16)
    proj_term = jnp.einsum("xc,fx->cf", normed, d_proj, preferred_element_type=jnp.float32)
    d_normed = jnp.einsum("fx,cf->xc", d_proj, proj_weight, preferred_element_type=jnp.float32)
    d_normed = d_normed + jnp.einsum(
        "xd,cd->xc", d_logits, gate_weight, preferred_element_type=jnp.float32
    )
    pair_grad = (
        norm_backward(d_normed, zhat, zscale, 1)
        .astype(jnp.bfloat16)
        .reshape(rows_here, length, width)
    )
    proj_sum, gate_sum, out_sum = lax.psum((proj_term, gate_term, out_term), "cells")
    factor = 1.0 / length
    return (pair_grad, proj_sum * factor, gate_sum * factor, out_sum * factor)


def solution(mesh):
    placed = (
        P(("groups", "cells"), None, None),
        P(("groups", "cells"), None),
        P("groups"),
        P(),
        P(),
        P(),
        P(),
        P(("groups", "cells"), None, None),
    )
    return jax.shard_map(
        local,
        mesh=mesh,
        in_specs=placed,
        out_specs=(
            P(("groups", "cells"), None, None),
            P("groups", None),
            P("groups", None),
            P("groups", None),
        ),
        check_vma=False,
    )
```

profile of v0, /device:TPU:0, one launch (start us, length us, event | category | flops | bytes accessed | tf_op | source)
XLA Modules:
  0.0 533.3 jit_solution(7304101476079198480)
XLA Ops:
  7.2 2.5 convert_reduce_fusion
  9.7 2.7 multiply_reduce_fusion.1
  12.6 5.0 fusion.12
  17.5 1.4 convolution_bitcast_fusion
  19.0 3.6 copy-done.1
  22.6 2.3 multiply_convert_fusion.3
  24.9 6.0 %reshape.157 = bf16[2,8,8,24,2,192]{5,4,3,2,1,0:T(2,128)(2,1)} reshape(bf16[128,9216]{1,0:T(8,128)(2,1)} %multiply_convert_fusion.3) | data formatting | bytes 4718592 | tf_op jit(solution)/shard_map/reshape | solution.py:41
  30.9 2.5 copy.21
  33.4 76.8 %all_to_all.47 = bf16[16,2,8,24,192]{4,3,2,1,0:T(8,128)(2,1)S(1)} all-to-all(bf16[16,2,8,24,192]{4,3,2,1,0:T(8,128)(2,1)S(1)} %bitcast.95), channel_id=1, replica_groups=mesh['groups'=2,'cells'=16] {'cells'}, dimensions={0} | all-to-all | bytes 4718592 | tf_op jit(solution)/shard_map/all_to_all | solution.py:45
  110.5 1.0 convolution_convert_fusion
  112.2 1.8 copy.25
  114.0 5.4 %all-to-all-start.1 = ((bf16[8,16,24,384]{3,2,0,1:T(8,128)(2,1)}), bf16[8,16,24,384]{3,2,0,1:T(8,128)(2,1)}, u32[]{:S(2)}, u32[]{:S(2)}) async-start(bf16[8,16,24,384]{3,2,0,1:T(8,128)(2,1)} %copy.25), calls=%async_computation.1 | async-start | bytes 4718592 | tf_op jit(solution)/shard_map/all_to_all | solution.py:51
  119.6 6.6 %fusion.7 = (bf16[9216,128]{1,0:T(8,128)(2,1)}, f32[9216,128]{1,0:T(8,128)}) fusion(bf16[24,384,128]{2,1,0:T(8,128)(2,1)} %param.15, f32[128]{0:T(128)S(1)} %get-tuple-element.11, f32[128]{0:T(128)S(1)} %get-tuple-element.10, pred[9216]{0:T(1024)(128)(4,1)S(1)} %eq.23, bf16[9216,128]{1,0:T(8,128)(2,1)} %copy-done.3, bf16[128,128]{1,0:T(8,128)(2,1)S(1)} %copy-done.14), kind=kOutput, calls=%fused_computation.13 | convolution fusion | flops 311427072 | bytes 11839488 | tf_op jit(solution)/shard_map/dot_general | solution.py:66
  126.3 38.7 %all-to-all-done.1 = bf16[8,16,24,384]{3,2,0,1:T(8,128)(2,1)} async-done(((bf16[8,16,24,384]{3,2,0,1:T(8,128)(2,1)}), bf16[8,16,24,384]{3,2,0,1:T(8,128)(2,1)}, u32[]{:S(2)}, u32[]{:S(2)}) %all-to-all-start.1) | async-done | bytes 2359328 | tf_op jit(solution)/shard_map/all_to_all | solution.py:51
  165.0 2.1 convert_reduce_fusion.1
  167.1 2.4 bitcast_reduce_fusion
  169.7 1.8 copy.27
  171.6 4.8 fusion.20
  176.3 1.8 reduce_sum.86
  178.2 2.9 fusion.19
  181.6 65.9 %all_to_all.48 = bf16[16,8,24,384]{3,2,1,0:T(8,128)(2,1)S(1)} all-to-all(bf16[16,8,24,384]{3,2,1,0:T(8,128)(2,1)S(1)} %bitcast.98), channel_id=1, replica_groups=mesh['groups'=2,'cells'=16] {'cells'}, dimensions={0} | all-to-all | bytes 4718592 | tf_op jit(solution)/shard_map/all_to_all | solution.py:80
  247.9 1.5 copy-done.7
  249.4 2.0 convolution_convert_fusion.1
  251.4 2.1 convolution_convert_fusion.2
  253.5 2.5 copy.30
  256.0 2.5 copy.31
  258.5 2.5 pad_maximum_fusion.1
  261.0 2.0 copy.32
  263.1 4.5 all-to-all-start.3
  267.6 2.9 fusion.22
  270.6 105.9 %psum.23 = f32[64,128]{1,0:T(8,128)S(1)} all-reduce(f32[64,128]{1,0:T(8,128)S(1)} %fusion.22), channel_id=1, replica_groups=mesh['groups'=2,'cells'=16] {'cells'}, use_global_device_ids=true, to_apply=%region_11.12 | all-reduce | flops 8192 | bytes 65536 | tf_op jit(solution)/shard_map/psum | solution.py:114
  377.1 5.4 %fusion.5 = bf16[9216,128]{1,0:T(8,128)(2,1)S(1)} fusion(f32[9216,128]{1,0:T(8,128)} %get-tuple-element.13, bf16[64,128]{1,0:T(8,128)(2,1)S(1)} %copy-done.12, bf16[9216,128]{1,0:T(8,128)(2,1)} %bitcast.104, f32[64,9216]{1,0:T(8,128)} %bitcast.89, f32[9216]{0:T(1024)S(1)} %div.42, f32[9216]{0:T(1024)S(1)} %rsqrt.25), kind=kOutput, calls=%fused_computation.9 | convolution fusion | flops 159842304 | bytes 11886592 | tf_op jit(solution)/shard_map/hx,hc->xc/dot_general | solution.py:62
  382.5 1.5 copy-done.8
  384.0 1.4 fusion.28
  385.5 2.2 copy.33
  387.7 3.5 convert_bitcast_fusion
  391.2 9.0 %copy.34 = f32[2,8,8,24,2,192]{5,4,3,2,1,0:T(2,128)} copy(f32[2,8,8,24,2,192]{5,3,4,1,2,0:T(8,128)} %convert_bitcast_fusion) | data formatting | bytes 9437184 | tf_op jit(solution)/shard_map/convert_element_type | solution.py:99
  400.2 9.3 %reshape.164 = f32[128,9216]{1,0:T(8,128)} reshape(f32[2,8,8,24,2,192]{5,4,3,2,1,0:T(2,128)} %copy.34) | data formatting | bytes 9437184 | tf_op jit(solution)/shard_map/convert_element_type | solution.py:99
  409.5 6.3 %multiply_convert_fusion.2 = (bf16[128,9216]{1,0:T(8,128)(2,1)S(1)}, bf16[128,9216]{1,0:T(8,128)(2,1)S(1)}) fusion(f32[128,9216]{1,0:T(8,128)} %reshape.164, f32[9216]{0:T(1024)S(1)} %mul.128, f32[256,9216]{1,0:T(8,128)} %copy-done.1), kind=kLoop, calls=%fused_computation.25 | loop fusion | flops 12976128 | bytes 18911232 | tf_op jit(solution)/shard_map/convert.7
  415.8 1.4 copy-done.10
  417.2 0.8 copy-done.11
  417.9 2.3 fusion.13
  420.3 4.0 fusion.14
  424.3 8.5 %fusion.27 = (f32[9216]{0:T(1024)S(1)}, f32[9216]{0:T(1024)S(1)}, f32[9216,128]{1,0:T(8,128)}) fusion(f32[9216]{0:T(1024)S(1)} %rsqrt.23, f32[9216]{0:T(1024)S(1)} %div.36, bf16[24,384,128]{2,1,0:T(8,128)(2,1)S(1)} %copy-done.2, f32[9216,128]{1,0:T(8,128)S(1)} %fusion.14, bf16[9216,128]{1,0:T(8,128)(2,1)S(1)} %copy-done.9, bf16[128,128]{1,0:T(8,128)(2,1)S(1)} %copy-done.14), kind=kOutput, calls=%fused_computation.67 | convolution fusion | flops 310228992 | bytes 14336000 | tf_op jit(solution)/shard_map/xd,cd->xc/dot_general | solution.py:106
  432.8 11.2 %multiply_convert_fusion = bf16[9216,128]{1,0:T(8,128)(2,1)} fusion(f32[9216,128]{1,0:T(8,128)} %get-tuple-element.16, bf16[24,384,128]{2,1,0:T(8,128)(2,1)S(1)} %copy-done.2, f32[9216]{0:T(1024)S(1)} %broadcast_multiply_fusion.2, f32[9216]{0:T(1024)S(1)} %broadcast_multiply_fusion.3, f32[9216]{0:T(1024)S(1)} %div.36, f32[9216]{0:T(1024)S(1)} %rsqrt.23), kind=kLoop, calls=%fused_computation.22 | loop fusion | flops 9437184 | bytes 9584640 | tf_op jit(solution)/shard_map/convert_element_type | solution.py:111
  444.0 79.5 %all-reduce.3.cloned.1.call-done = (f32[128,256]{1,0:T(8,128)}, f32[128,128]{1,0:T(8,128)}) async-done(((f32[128,256]{1,0:T(8,128)}, f32[128,128]{1,0:T(8,128)}), (f32[128,256]{1,0:T(8,128)}, f32[128,128]{1,0:T(8,128)})) %all-reduce.3.cloned.1.call-update) | async-done | bytes 196624 | tf_op jit(solution)/shard_map/psum | solution.py:114
  523.5 1.6 broadcast_multiply_fusion
  525.0 1.5 broadcast_multiply_fusion.1
  (55 shorter events, 3.1 us)
Async XLA Ops:
  7.2 10.4 %copy-start = (bf16[128,256]{1,0:T(8,128)(2,1)S(1)}, bf16[128,256]{1,0:T(8,128)(2,1)}, u32[]{:S(2)}) copy-start(bf16[128,256]{1,0:T(8,128)(2,1)} %param.11) | copy-start | bytes 196612
  7.2 2.6 copy-start.2
  7.2 5.3 copy-start.13
  17.5 1.4 copy-start.3
  19.0 3.6 copy-start.1
  110.5 1.6 copy-start.6
  114.0 5.4 %copy-start.15 = (s32[384]{0:T(512)S(1)}, s32[384]{0:T(512)}, u32[]{:S(2)}) copy-start(s32[384]{0:T(512)} %param.10) | copy-start | bytes 4612
  114.0 5.6 %copy-start.16 = (f32[2,128]{1,0:T(2,128)S(1)}, f32[2,128]{1,0:T(2,128)}, u32[]{:S(2)}) copy-start(f32[2,128]{1,0:T(2,128)} %param.13) | copy-start | bytes 3076
  114.0 5.6 %copy-start.14 = (bf16[128,128]{1,0:T(8,128)(2,1)S(1)}, bf16[128,128]{1,0:T(8,128)(2,1)}, u32[]{:S(2)}) copy-start(bf16[128,128]{1,0:T(8,128)(2,1)} %param.12) | copy-start | bytes 98308
  114.0 51.0 %all-to-all-start.1 = ((bf16[8,16,24,384]{3,2,0,1:T(8,128)(2,1)}), bf16[8,16,24,384]{3,2,0,1:T(8,128)(2,1)}, u32[]{:S(2)}, u32[]{:S(2)}) async-start(bf16[8,16,24,384]{3,2,0,1:T(8,128)(2,1)} %copy.25), calls=%async_computation.1 | async-start | bytes 4718592 | tf_op jit(solution)/shard_map/all_to_all | solution.py:51
  169.7 1.9 copy-start.12
  247.5 1.9 copy-start.7
  263.1 122.4 %all-to-all-start.3 = ((bf16[2,8,16,24,192]{4,3,1,0,2:T(8,128)(2,1)}), bf16[2,8,16,24,192]{4,3,1,0,2:T(8,128)(2,1)}, u32[]{:S(2)}, u32[]{:S(2)}) async-start(bf16[2,8,16,24,192]{4,3,1,0,2:T(8,128)(2,1)} %copy.32), calls=%async_computation.3 | async-start | bytes 6291456 | tf_op jit(solution)/shard_map/all_to_all | solution.py:90
  267.6 255.9 %all-reduce.3.cloned.1.call-start = ((), (), s32[]{:S(2)}) async-start(), calls=%async_computation.4 | async-start | bytes 393216 | tf_op jit(solution)/shard_map/psum | solution.py:114
  377.1 6.9 %copy-start.4 = (bf16[9216,128]{1,0:T(8,128)(2,1)S(1)}, bf16[9216,128]{1,0:T(8,128)(2,1)}, u32[]{:S(2)}) copy-start(bf16[9216,128]{1,0:T(8,128)(2,1)} %copy-done.3) | copy-start | bytes 7077892
  382.5 1.5 copy-start.8
  409.5 8.5 %copy-start.5 = (bf16[9216,128]{1,0:T(8,128)(2,1)S(1)}, bf16[9216,128]{1,0:T(8,128)(2,1)}, u32[]{:S(2)}) copy-start(bf16[9216,128]{1,0:T(8,128)(2,1)} %copy-done.3) | copy-start | bytes 7077892
  415.8 1.4 copy-start.10
  415.8 2.2 copy-start.11
  420.3 4.0 copy-start.9
Sparse Core Ops, SparseCore 0:
  432.9 90.5 all-reduce.2
where the time goes:
time: 535 us; the launch traced here: 533 us
  blocking collectives  249 us (47%)
  waiting for transfers between devices  118 us (22%)
  local copies, waits for them, and re-layouts  50.5 us (9%)
  other arithmetic  49.2 us (9%)
  matrix products  42.5 us (8%)
  between operations  14.4 us (3%)
  starting transfers between devices  9.93 us (2%)
    psum x1, blocking collectives, local(): lax.psum((proj_term, gate_term, out_term), 'cells')  106 us
    psum x1, waiting for transfers between devices, local(): lax.psum((proj_term, gate_term, out_term), 'cells')  79.5 us
    all_to_all x1, blocking collectives, local(): lax.all_to_all(outgoing, 'cells', split_axis=0, concat_axis=3, tiled=True)  76.8 us
    all_to_all x1, blocking collectives, local(): lax.all_to_all(doubled.reshape(devices, per_device, rows_here, length), '...  65.9 us
    all_to_all x1, waiting for transfers between devices, local(): lax.all_to_all(partial_value.reshape(per_device, devices, rows_here, leng...  38.7 us
    convert_element_type x2, local copies, waits for them, and re-layouts, local(): jnp.transpose(returned, (0, 2, 1, 4, 3, 5)).reshape(2 * hidden, count)  18.3 us
    convert_element_type x1, other arithmetic, local(): pair_grad = norm_backward(d_normed, zhat, zscale, 1).astype(jnp.bfloat16)...  11.2 us
  transfers between devices with their start and end apart: 3, of which 2 were waited for; matrix products, arithmetic and copies ran while one was open for 5% of the time, Pallas kernels for 0%

commit v1 on v0

--- a/solution.py
+++ b/solution.py
@@ -42,7 +42,12 @@
     outgoing = jnp.transpose(outgoing, (1, 4, 0, 2, 3, 5)).reshape(
         devices, 2, per_device, rows_here, halfway
     )
-    arrived = lax.all_to_all(outgoing, "cells", split_axis=0, concat_axis=3, tiled=True)
+    arrived = jnp.concatenate(
+        lax.all_to_all(
+            jnp.stack(jnp.split(outgoing, lax.axis_size("cells"), axis=0)), "cells", 0, 0
+        ),
+        axis=3,
+    )
     left_half = arrived[0, 0]
     right_half = arrived[0, 1]
     partial_value = jnp.einsum(

time: 535 us -> 536 us (level)
    unnamed x34 -> x49, local copies, waits for them, and re-layouts: 9.5 us -> 10.7 us
where the time goes in v1:
time: 536 us; the launch traced here: 535 us
  blocking collectives  249 us (46%)
  waiting for transfers between devices  118 us (22%)
  local copies, waits for them, and re-layouts  51.7 us (10%)
  other arithmetic  49.2 us (9%)
  matrix products  42.5 us (8%)
  between operations  14.5 us (3%)
  starting transfers between devices  9.93 us (2%)
    psum x1, blocking collectives, local(): lax.psum((proj_term, gate_term, out_term), 'cells')  106 us
    psum x1, waiting for transfers between devices, local(): lax.psum((proj_term, gate_term, out_term), 'cells')  79.5 us
    all_to_all x1, blocking collectives, local(): lax.all_to_all(jnp.stack(jnp.split(outgoing, lax.axis_size('cells'), axis...  76.8 us
    all_to_all x1, blocking collectives, local(): lax.all_to_all(doubled.reshape(devices, per_device, rows_here, length), '...  65.9 us
    all_to_all x1, waiting for transfers between devices, local(): lax.all_to_all(partial_value.reshape(per_device, devices, rows_here, leng...  38.7 us
    convert_element_type x2, local copies, waits for them, and re-layouts, local(): jnp.transpose(returned, (0, 2, 1, 4, 3, 5)).reshape(2 * hidden, count)  18.3 us
    convert_element_type x1, other arithmetic, local(): pair_grad = norm_backward(d_normed, zhat, zscale, 1).astype(jnp.bfloat16)...  11.2 us
    unnamed x49, local copies, waits for them, and re-layouts  10.7 us
  transfers between devices with their start and end apart: 3, of which 2 were waited for; matrix products, arithmetic and copies ran while one was open for 5% of the time, Pallas kernels for 0%

profile of v1, /device:TPU:0, one launch (start us, length us, event | category | flops | bytes accessed | tf_op | source)
XLA Modules:
  0.0 534.7 jit_solution(16655016404312911022)
XLA Ops:
  7.2 2.5 convert_reduce_fusion
  9.7 2.7 multiply_reduce_fusion.1
  12.6 5.0 fusion.12
  17.5 1.4 convolution_bitcast_fusion
  19.0 3.6 copy-done.1
  22.6 2.3 multiply_convert_fusion.3
  24.9 6.0 %reshape.163 = bf16[2,8,8,24,2,192]{5,4,3,2,1,0:T(2,128)(2,1)} reshape(bf16[128,9216]{1,0:T(8,128)(2,1)} %multiply_convert_fusion.3) | data formatting | bytes 4718592 | tf_op jit(solution)/shard_map/reshape | solution.py:41
  30.9 2.5 copy.36
  33.7 76.8 %all_to_all.34 = bf16[16,1,2,8,24,192]{5,4,3,2,1,0:T(8,128)(2,1)S(1)} all-to-all(bf16[16,1,2,8,24,192]{5,4,3,2,1,0:T(8,128)(2,1)S(1)} %fusion.25), channel_id=1, replica_groups=mesh['groups'=2,'cells'=16] {'cells'}, dimensions={0} | all-to-all | bytes 4718592 | tf_op jit(solution)/shard_map/all_to_all | solution.py:46
  110.9 1.6 copy-done.6
  112.5 1.0 convolution_convert_fusion
  113.5 1.8 copy.40
  115.3 5.4 %all-to-all-start.1 = ((bf16[8,16,24,384]{3,2,0,1:T(8,128)(2,1)}), bf16[8,16,24,384]{3,2,0,1:T(8,128)(2,1)}, u32[]{:S(2)}, u32[]{:S(2)}) async-start(bf16[8,16,24,384]{3,2,0,1:T(8,128)(2,1)} %copy.40), calls=%async_computation.1 | async-start | bytes 4718592 | tf_op jit(solution)/shard_map/all_to_all | solution.py:56
  121.0 6.6 %fusion.7 = (bf16[9216,128]{1,0:T(8,128)(2,1)}, f32[9216,128]{1,0:T(8,128)}) fusion(bf16[24,384,128]{2,1,0:T(8,128)(2,1)} %param.15, f32[128]{0:T(128)S(1)} %get-tuple-element.11, f32[128]{0:T(128)S(1)} %get-tuple-element.10, pred[9216]{0:T(1024)(128)(4,1)S(1)} %eq.23, bf16[9216,128]{1,0:T(8,128)(2,1)} %copy-done.3, bf16[128,128]{1,0:T(8,128)(2,1)S(1)} %copy-done.14), kind=kOutput, calls=%fused_computation.13 | convolution fusion | flops 311427072 | bytes 11839488 | tf_op jit(solution)/shard_map/dot_general | solution.py:71
  127.6 38.7 %all-to-all-done.1 = bf16[8,16,24,384]{3,2,0,1:T(8,128)(2,1)} async-done(((bf16[8,16,24,384]{3,2,0,1:T(8,128)(2,1)}), bf16[8,16,24,384]{3,2,0,1:T(8,128)(2,1)}, u32[]{:S(2)}, u32[]{:S(2)}) %all-to-all-start.1) | async-done | bytes 2359328 | tf_op jit(solution)/shard_map/all_to_all | solution.py:56
  166.3 2.1 convert_reduce_fusion.1
  168.4 2.4 bitcast_reduce_fusion
  171.1 1.8 copy.42
  172.9 4.8 fusion.20
  177.7 1.8 reduce_sum.86
  179.5 2.9 fusion.19
  183.0 65.9 %all_to_all.35 = bf16[16,8,24,384]{3,2,1,0:T(8,128)(2,1)S(1)} all-to-all(bf16[16,8,24,384]{3,2,1,0:T(8,128)(2,1)S(1)} %bitcast.175), channel_id=1, replica_groups=mesh['groups'=2,'cells'=16] {'cells'}, dimensions={0} | all-to-all | bytes 4718592 | tf_op jit(solution)/shard_map/all_to_all | solution.py:85
  249.2 1.5 copy-done.7
  250.8 2.0 convolution_convert_fusion.1
  252.8 2.1 convolution_convert_fusion.2
  254.9 2.5 copy.45
  257.4 2.5 copy.46
  259.9 2.5 pad_maximum_fusion.1
  262.4 2.0 copy.47
  264.4 4.5 all-to-all-start.3
  269.0 2.9 fusion.22
  271.9 105.9 %psum.23 = f32[64,128]{1,0:T(8,128)S(1)} all-reduce(f32[64,128]{1,0:T(8,128)S(1)} %fusion.22), channel_id=1, replica_groups=mesh['groups'=2,'cells'=16] {'cells'}, use_global_device_ids=true, to_apply=%region_11.12 | all-reduce | flops 8192 | bytes 65536 | tf_op jit(solution)/shard_map/psum | solution.py:119
  378.5 5.4 %fusion.5 = bf16[9216,128]{1,0:T(8,128)(2,1)S(1)} fusion(f32[9216,128]{1,0:T(8,128)} %get-tuple-element.13, bf16[64,128]{1,0:T(8,128)(2,1)S(1)} %copy-done.12, bf16[9216,128]{1,0:T(8,128)(2,1)} %bitcast.181, f32[64,9216]{1,0:T(8,128)} %bitcast.151, f32[9216]{0:T(1024)S(1)} %div.42, f32[9216]{0:T(1024)S(1)} %rsqrt.25), kind=kOutput, calls=%fused_computation.9 | convolution fusion | flops 159842304 | bytes 11886592 | tf_op jit(solution)/shard_map/hx,hc->xc/dot_general | solution.py:67
  383.9 1.5 copy-done.8
  385.4 1.4 fusion.44
  386.8 2.2 copy.48
  389.0 3.5 convert_bitcast_fusion
  392.5 9.0 %copy.49 = f32[2,8,8,24,2,192]{5,4,3,2,1,0:T(2,128)} copy(f32[2,8,8,24,2,192]{5,3,4,1,2,0:T(8,128)} %convert_bitcast_fusion) | data formatting | bytes 9437184 | tf_op jit(solution)/shard_map/convert_element_type | solution.py:104
  401.6 9.3 %reshape.172 = f32[128,9216]{1,0:T(8,128)} reshape(f32[2,8,8,24,2,192]{5,4,3,2,1,0:T(2,128)} %copy.49) | data formatting | bytes 9437184 | tf_op jit(solution)/shard_map/convert_element_type | solution.py:104
  410.8 6.3 %multiply_convert_fusion.2 = (bf16[128,9216]{1,0:T(8,128)(2,1)S(1)}, bf16[128,9216]{1,0:T(8,128)(2,1)S(1)}) fusion(f32[128,9216]{1,0:T(8,128)} %reshape.172, f32[9216]{0:T(1024)S(1)} %mul.128, f32[256,9216]{1,0:T(8,128)} %copy-done.1), kind=kLoop, calls=%fused_computation.25 | loop fusion | flops 12976128 | bytes 18911232 | tf_op jit(solution)/shard_map/convert.7
  417.1 1.4 copy-done.10
  419.3 2.3 fusion.13
  421.6 4.0 fusion.14
  425.6 8.5 %fusion.43 = (f32[9216]{0:T(1024)S(1)}, f32[9216]{0:T(1024)S(1)}, f32[9216,128]{1,0:T(8,128)}) fusion(f32[9216]{0:T(1024)S(1)} %rsqrt.23, f32[9216]{0:T(1024)S(1)} %div.36, bf16[24,384,128]{2,1,0:T(8,128)(2,1)S(1)} %copy-done.2, f32[9216,128]{1,0:T(8,128)S(1)} %fusion.14, bf16[9216,128]{1,0:T(8,128)(2,1)S(1)} %copy-done.9, bf16[128,128]{1,0:T(8,128)(2,1)S(1)} %copy-done.14), kind=kOutput, calls=%fused_computation.99 | convolution fusion | flops 310228992 | bytes 14336000 | tf_op jit(solution)/shard_map/xd,cd->xc/dot_general | solution.py:111
  434.2 11.2 %multiply_convert_fusion = bf16[9216,128]{1,0:T(8,128)(2,1)} fusion(f32[9216,128]{1,0:T(8,128)} %get-tuple-element.16, bf16[24,384,128]{2,1,0:T(8,128)(2,1)S(1)} %copy-done.2, f32[9216]{0:T(1024)S(1)} %broadcast_multiply_fusion.2, f32[9216]{0:T(1024)S(1)} %broadcast_multiply_fusion.3, f32[9216]{0:T(1024)S(1)} %div.36, f32[9216]{0:T(1024)S(1)} %rsqrt.23), kind=kLoop, calls=%fused_computation.22 | loop fusion | flops 9437184 | bytes 9584640 | tf_op jit(solution)/shard_map/convert_element_type | solution.py:116
  445.4 79.5 %all-reduce.3.cloned.1.call-done = (f32[128,256]{1,0:T(8,128)}, f32[128,128]{1,0:T(8,128)}) async-done(((f32[128,256]{1,0:T(8,128)}, f32[128,128]{1,0:T(8,128)}), (f32[128,256]{1,0:T(8,128)}, f32[128,128]{1,0:T(8,128)})) %all-reduce.3.cloned.1.call-update) | async-done | bytes 196624 | tf_op jit(solution)/shard_map/psum | solution.py:119
  524.8 1.6 broadcast_multiply_fusion
  526.4 1.5 broadcast_multiply_fusion.1
  (71 shorter events, 3.5 us)
Async XLA Ops:
  7.2 10.4 %copy-start = (bf16[128,256]{1,0:T(8,128)(2,1)S(1)}, bf16[128,256]{1,0:T(8,128)(2,1)}, u32[]{:S(2)}) copy-start(bf16[128,256]{1,0:T(8,128)(2,1)} %param.11) | copy-start | bytes 196612
  7.2 2.6 copy-start.2
  7.2 5.3 copy-start.13
  17.5 1.4 copy-start.3
  19.0 3.6 copy-start.1
  110.9 1.6 copy-start.6
  115.3 5.4 %copy-start.15 = (s32[384]{0:T(512)S(1)}, s32[384]{0:T(512)}, u32[]{:S(2)}) copy-start(s32[384]{0:T(512)} %param.10) | copy-start | bytes 4612
  115.3 5.6 %copy-start.16 = (f32[2,128]{1,0:T(2,128)S(1)}, f32[2,128]{1,0:T(2,128)}, u32[]{:S(2)}) copy-start(f32[2,128]{1,0:T(2,128)} %param.13) | copy-start | bytes 3076
  115.3 5.6 %copy-start.14 = (bf16[128,128]{1,0:T(8,128)(2,1)S(1)}, bf16[128,128]{1,0:T(8,128)(2,1)}, u32[]{:S(2)}) copy-start(bf16[128,128]{1,0:T(8,128)(2,1)} %param.12) | copy-start | bytes 98308
  115.3 51.0 %all-to-all-start.1 = ((bf16[8,16,24,384]{3,2,0,1:T(8,128)(2,1)}), bf16[8,16,24,384]{3,2,0,1:T(8,128)(2,1)}, u32[]{:S(2)}, u32[]{:S(2)}) async-start(bf16[8,16,24,384]{3,2,0,1:T(8,128)(2,1)} %copy.40), calls=%async_computation.1 | async-start | bytes 4718592 | tf_op jit(solution)/shard_map/all_to_all | solution.py:56
  170.8 2.1 copy-start.12
  248.9 1.9 copy-start.7
  264.4 122.4 %all-to-all-start.3 = ((bf16[2,8,16,24,192]{4,3,1,0,2:T(8,128)(2,1)}), bf16[2,8,16,24,192]{4,3,1,0,2:T(8,128)(2,1)}, u32[]{:S(2)}, u32[]{:S(2)}) async-start(bf16[2,8,16,24,192]{4,3,1,0,2:T(8,128)(2,1)} %copy.47), calls=%async_computation.3 | async-start | bytes 6291456 | tf_op jit(solution)/shard_map/all_to_all | solution.py:95
  268.9 255.9 %all-reduce.3.cloned.1.call-start = ((), (), s32[]{:S(2)}) async-start(), calls=%async_computation.4 | async-start | bytes 393216 | tf_op jit(solution)/shard_map/psum | solution.py:119
  378.5 6.9 %copy-start.4 = (bf16[9216,128]{1,0:T(8,128)(2,1)S(1)}, bf16[9216,128]{1,0:T(8,128)(2,1)}, u32[]{:S(2)}) copy-start(bf16[9216,128]{1,0:T(8,128)(2,1)} %copy-done.3) | copy-start | bytes 7077892
  383.9 1.5 copy-start.8
  410.8 8.5 %copy-start.5 = (bf16[9216,128]{1,0:T(8,128)(2,1)S(1)}, bf16[9216,128]{1,0:T(8,128)(2,1)}, u32[]{:S(2)}) copy-start(bf16[9216,128]{1,0:T(8,128)(2,1)} %copy-done.3) | copy-start | bytes 7077892
  417.1 1.4 copy-start.10
  417.1 2.2 copy-start.11
  421.6 4.0 copy-start.9
Sparse Core Ops, SparseCore 0:
  434.3 90.5 all-reduce.2
